TPU v7x, 32 devices: a whole 2x2x4 slice. The times are simulated.
32 devices in a mesh: dp: 8 (over z, y), head: 4 (over x, core).
Axes of the slice: x: 2, y: 2, z: 4, core: 2. Of those that a mesh axis runs over, the one named last changes fastest.
Arguments:
- tokens: bfloat16 [8, 6312, 768], P('dp', 'head'), may hold values from -6 to 6
- frames: int32 [8], P('dp'), may hold values from 4 to 16
- text_mask: int32 [8, 40], P('dp'), may hold values 0 or 1
- latents: bfloat16 [8, 128, 768], P('dp'), may hold values from -6 to 6
- cross_q: bfloat16 [768, 768], P('head'), may hold values from -0.21875 to 0.21875
- cross_kv: bfloat16 [2, 768, 768], P(None, 'head'), may hold values from -0.21875 to 0.21875
- cross_out: bfloat16 [768, 768], P('head'), may hold values from -3.5 to 3.5
- cross_up: bfloat16 [768, 3072], P(None, 'head'), may hold values from -0.21875 to 0.21875
- cross_down: bfloat16 [3072, 768], P('head'), may hold values from -0.109375 to 0.109375
- self_qkv: bfloat16 [3, 768, 768], P(None, 'head'), may hold values from -0.21875 to 0.21875
- self_out: bfloat16 [768, 768], P('head'), may hold values from -0.875 to 0.875
- self_up: bfloat16 [768, 3072], P(None, 'head'), may hold values from -0.21875 to 0.21875
- self_down: bfloat16 [3072, 768], P('head'), may hold values from -0.109375 to 0.109375
- head_bias: float32 [2, 2, 768], P(None, None, 'head'), may hold values from -1.8 to 1.8
- up_bias: float32 [2, 3072], P(None, 'head'), may hold values from -1.8 to 1.8
- out_bias: float32 [2, 2, 768], replicated, may hold values from -1.8 to 1.8
- norm_gain: float32 [5, 768], replicated, may hold values from 0.5 to 1.5
- norm_bias: float32 [5, 768], replicated, may hold values from -1.8 to 1.8
- latents_cot: float32 [8, 128, 768], P('dp'), may hold values from -6 to 6
Outputs:
- latents_out: float32 [8, 128, 768], P('dp')
- grad_tokens: bfloat16 [8, 6312, 768], P('dp', 'head')
- grad_latents: float32 [8, 128, 768], P('dp')
- grad_cross_q: float32 [768, 768], P('head', 'dp')
- grad_cross_kv: float32 [2, 768, 768], P(None, 'head', 'dp')
- grad_cross_out: float32 [768, 768], P('head', 'dp')
- grad_cross_up: float32 [768, 3072], P('dp', 'head')
- grad_cross_down: float32 [3072, 768], P('head', 'dp')
- grad_self_qkv: float32 [3, 768, 768], P(None, 'head', 'dp')
- grad_self_out: float32 [768, 768], P('head', 'dp')
- grad_self_up: float32 [768, 3072], P('dp', 'head')
- grad_self_down: float32 [3072, 768], P('head', 'dp')
- grad_head_bias: float32 [2, 2, 768], P(None, None, 'head')
- grad_up_bias: float32 [2, 3072], P(None, 'head')
- grad_out_bias: float32 [2, 2, 768], P(None, None, 'head')
- grad_norm_gain: float32 [5, 768], P(None, 'head')
- grad_norm_bias: float32 [5, 768], P(None, 'head')
Inputs may be any that keep to these rules, and one draw needn't show every extreme that they name: The patches of frames at or after frames[c] are padding.
All inputs are finite; a program needn't handle non-finite values. No bound on the sum of `text_mask` on one device may be relied on, other than what follows from the above.
Results may differ from a plain program's by a relative error of at most 0.018.
Values may be sent and summed in bfloat16 or wider, within the bound.
A program may use at most 128 MiB of HBM per device.

v0:
```python
from functools import partial
import jax
import jax.numpy as jnp
from jax import lax
from jax.sharding import PartitionSpec as P

HD = 64
P_SIZE = 392
F_MAX = 16
EPSILON = 1e-05
NEGATIVE = -1e30


def normed(tensor, gain_row, shift_row):
    row_mean = jnp.mean(tensor, axis=-1, keepdims=True)
    centered = tensor - row_mean
    spread = jnp.mean(centered * centered, axis=-1, keepdims=True)
    return centered * lax.rsqrt(spread + EPSILON) * gain_row + shift_row


def share_of(tensor, head_index, head_width):
    return lax.dynamic_slice_in_dim(tensor, head_index * head_width, head_width, tensor.ndim - 1)


def split_heads(tensor, heads_here):
    return tensor.reshape(
        tensor.shape[0], tensor.shape[1], heads_here, tensor.shape[2] // heads_here
    )


def merge_heads(tensor):
    return tensor.reshape(tensor.shape[0], tensor.shape[1], tensor.shape[2] * tensor.shape[3])


def join_heads(partial_sum):
    return lax.psum(partial_sum.astype(jnp.bfloat16), "head").astype(jnp.float32)


def join_back(partial_sum):
    return lax.psum(partial_sum.astype(jnp.bfloat16), "head").astype(jnp.float32)


def scores_of(queries, key_rows, usable):
    scores = jnp.einsum("qhe,khe->hqk", queries, key_rows, preferred_element_type=jnp.float32)
    return jnp.where(usable[None, None, :], scores, NEGATIVE)


def attend_parts(parts):
    queries, key_rows, values, usable = parts
    scores = scores_of(queries, key_rows, usable)
    row_max = jnp.max(scores, axis=-1, keepdims=True)
    powers = jnp.exp(scores - row_max)
    totals = jnp.sum(powers, axis=-1, keepdims=True)
    chances = (powers / totals).astype(jnp.bfloat16)
    mixture = jnp.einsum("hqk,khe->qhe", chances, values, preferred_element_type=jnp.float32)
    return (mixture.astype(jnp.bfloat16), row_max, totals)


def back_parts(parts):
    queries, key_rows, values, usable, row_max, totals, grad_mix = parts
    scores = scores_of(queries, key_rows, usable)
    chances = jnp.exp(scores - row_max) / totals
    rounded = chances.astype(jnp.bfloat16)
    grad_values = jnp.einsum(
        "hqk,qhe->khe", rounded, grad_mix, preferred_element_type=jnp.float32
    ).astype(jnp.bfloat16)
    grad_chances = jnp.einsum("qhe,khe->hqk", grad_mix, values, preferred_element_type=jnp.float32)
    inner_sum = jnp.sum(chances * grad_chances, axis=-1, keepdims=True)
    grad_scores = (chances * (grad_chances - inner_sum)).astype(jnp.bfloat16)
    grad_queries = jnp.einsum(
        "hqk,khe->qhe", grad_scores, key_rows, preferred_element_type=jnp.float32
    ).astype(jnp.bfloat16)
    grad_keys = jnp.einsum(
        "hqk,qhe->khe", grad_scores, queries, preferred_element_type=jnp.float32
    ).astype(jnp.bfloat16)
    return (grad_queries, grad_keys, grad_values)


def feed_forward(tensor, gain_row, shift_row, weight_up, bias_up, weight_down):
    hidden = normed(tensor, gain_row, shift_row).astype(jnp.bfloat16)
    pre_act = (
        jnp.einsum("cnd,df->cnf", hidden, weight_up, preferred_element_type=jnp.float32) + bias_up
    )
    activation = jax.nn.gelu(pre_act, approximate=True).astype(jnp.bfloat16)
    partial_sum = jnp.einsum(
        "cnf,fd->cnd", activation, weight_down, preferred_element_type=jnp.float32
    )
    return (join_heads(partial_sum), (hidden, pre_act, activation))


def feed_back(tensor, gain_row, shift_row, weight_up, weight_down, saved_acts, grad_out):
    hidden, pre_act, activation = saved_acts
    grad_branch = grad_out.astype(jnp.bfloat16)
    grad_weight_down = jnp.einsum(
        "cnf,cnd->fd", activation, grad_branch, preferred_element_type=jnp.float32
    )
    grad_act = jnp.einsum(
        "cnd,fd->cnf", grad_branch, weight_down, preferred_element_type=jnp.float32
    )
    unused, gelu_pull = jax.vjp(partial(jax.nn.gelu, approximate=True), pre_act)
    grad_pre = gelu_pull(grad_act)[0].astype(jnp.bfloat16)
    grad_weight_up = jnp.einsum("cnd,cnf->df", hidden, grad_pre, preferred_element_type=jnp.float32)
    grad_bias_up = jnp.sum(grad_pre.astype(jnp.float32), axis=(0, 1))
    grad_hidden = join_back(
        jnp.einsum("cnf,df->cnd", grad_pre, weight_up, preferred_element_type=jnp.float32)
    )
    unused_too, norm_pull = jax.vjp(normed, tensor, gain_row, shift_row)
    grad_tensor, grad_gain, grad_shift = norm_pull(grad_hidden)
    return (grad_tensor, grad_weight_up, grad_bias_up, grad_weight_down, grad_gain, grad_shift)


def local(
    tokens,
    frames,
    text_mask,
    latents,
    cross_q,
    cross_kv,
    cross_out,
    cross_up,
    cross_down,
    self_qkv,
    self_out,
    self_up,
    self_down,
    head_bias,
    up_bias,
    out_bias,
    norm_gain,
    norm_bias,
    latents_cot,
):
    head_index = lax.axis_index("head")
    head_width = cross_q.shape[0]
    heads_here = head_width // HD
    scaling = HD ** (-0.5)
    clips_here = tokens.shape[0]
    rows_here = tokens.shape[1]
    length = rows_here * lax.axis_size("head")
    position = jnp.arange(length, dtype=jnp.int32)
    text_full = jnp.concatenate(
        [jnp.zeros((clips_here, F_MAX * P_SIZE), jnp.int32), text_mask], axis=1
    )
    usable = (position[None, :] < frames[:, None] * P_SIZE) | (text_full == 1)
    gathered, weights_whole = (
        lax.all_gather(tokens, "head", axis=1, tiled=True),
        lax.all_gather(cross_kv, "head", axis=1, tiled=True),
    )
    full_rows = gathered.astype(jnp.float32)
    row_mean = jnp.mean(full_rows, axis=-1, keepdims=True)
    centered = full_rows - row_mean
    inverse = lax.rsqrt(jnp.mean(centered * centered, axis=-1, keepdims=True) + EPSILON)
    inputs = (centered * inverse * norm_gain[0] + norm_bias[0]).astype(jnp.bfloat16)
    key_value = jnp.einsum("cld,kwd->clkw", inputs, cross_kv, preferred_element_type=jnp.float32)
    key_rows = key_value[:, :, 0].astype(jnp.bfloat16)
    cross_values = (key_value[:, :, 1] + head_bias[0, 1]).astype(jnp.bfloat16)
    start_state = latents.astype(jnp.float32)
    latent_norm = normed(start_state, norm_gain[1], norm_bias[1]).astype(jnp.bfloat16)
    cross_queries = (
        (
            jnp.einsum("cnd,wd->cnw", latent_norm, cross_q, preferred_element_type=jnp.float32)
            + head_bias[0, 0]
        )
        * scaling
    ).astype(jnp.bfloat16)
    cross_parts = (
        split_heads(cross_queries, heads_here),
        split_heads(key_rows, heads_here),
        split_heads(cross_values, heads_here),
        usable,
    )
    cross_mix, cross_max, cross_totals = lax.map(attend_parts, cross_parts)
    cross_flat = merge_heads(cross_mix)
    after_cross = (
        start_state
        + join_heads(
            jnp.einsum("cnw,wd->cnd", cross_flat, cross_out, preferred_element_type=jnp.float32)
        )
        + out_bias[0, 0]
    )
    cross_branch, cross_saved = feed_forward(
        after_cross, norm_gain[2], norm_bias[2], cross_up, up_bias[0], cross_down
    )
    after_mlp = after_cross + cross_branch + out_bias[0, 1]
    self_norm = normed(after_mlp, norm_gain[3], norm_bias[3]).astype(jnp.bfloat16)
    triple = jnp.einsum("cnd,kwd->cnkw", self_norm, self_qkv, preferred_element_type=jnp.float32)
    self_queries = ((triple[:, :, 0] + head_bias[1, 0]) * scaling).astype(jnp.bfloat16)
    self_keys = triple[:, :, 1].astype(jnp.bfloat16)
    self_values = (triple[:, :, 2] + head_bias[1, 1]).astype(jnp.bfloat16)
    everyone = jnp.ones((clips_here, self_keys.shape[1]), dtype=bool)
    self_parts = (
        split_heads(self_queries, heads_here),
        split_heads(self_keys, heads_here),
        split_heads(self_values, heads_here),
        everyone,
    )
    self_mix, self_max, self_totals = lax.map(attend_parts, self_parts)
    self_flat = merge_heads(self_mix)
    after_self = (
        after_mlp
        + join_heads(
            jnp.einsum("cnw,wd->cnd", self_flat, self_out, preferred_element_type=jnp.float32)
        )
        + out_bias[1, 0]
    )
    self_branch, self_saved = feed_forward(
        after_self, norm_gain[4], norm_bias[4], self_up, up_bias[1], self_down
    )
    latents_out = after_self + self_branch + out_bias[1, 1]
    bias_self_mlp = jnp.sum(latents_cot, axis=(0, 1))
    grad_ln_four, grad_self_up, upbias_self, grad_self_down, gain_four, shift_four = feed_back(
        after_self, norm_gain[4], norm_bias[4], self_up, self_down, self_saved, latents_cot
    )
    grad_state = latents_cot + grad_ln_four
    bias_self_attn = jnp.sum(grad_state, axis=(0, 1))
    grad_attn_in = grad_state.astype(jnp.bfloat16)
    grad_self_out = jnp.einsum(
        "cnw,cnd->wd", self_flat, grad_attn_in, preferred_element_type=jnp.float32
    )
    grad_mix = jnp.einsum(
        "cnd,wd->cnw", grad_attn_in, self_out, preferred_element_type=jnp.float32
    ).astype(jnp.bfloat16)
    self_grads = lax.map(
        back_parts, self_parts + (self_max, self_totals, split_heads(grad_mix, heads_here))
    )
    grad_query_scaled = (merge_heads(self_grads[0]).astype(jnp.float32) * scaling).astype(
        jnp.bfloat16
    )
    grad_triple = jnp.stack(
        [grad_query_scaled, merge_heads(self_grads[1]), merge_heads(self_grads[2])], axis=2
    )
    grad_self_qkv = jnp.einsum(
        "cnd,cnkw->kwd", self_norm, grad_triple, preferred_element_type=jnp.float32
    )
    bias_self_q = jnp.sum(grad_triple[:, :, 0].astype(jnp.float32), axis=(0, 1))
    bias_self_v = jnp.sum(grad_triple[:, :, 2].astype(jnp.float32), axis=(0, 1))
    grad_self_in = join_back(
        jnp.einsum("cnkw,kwd->cnd", grad_triple, self_qkv, preferred_element_type=jnp.float32)
    )
    unused, norm_pull = jax.vjp(normed, after_mlp, norm_gain[3], norm_bias[3])
    grad_ln_three, gain_three, shift_three = norm_pull(grad_self_in)
    grad_state = grad_state + grad_ln_three
    bias_cross_mlp = jnp.sum(grad_state, axis=(0, 1))
    grad_ln_two, grad_cross_up, upbias_cross, grad_cross_down, gain_two, shift_two = feed_back(
        after_cross, norm_gain[2], norm_bias[2], cross_up, cross_down, cross_saved, grad_state
    )
    grad_state = grad_state + grad_ln_two
    bias_cross_attn = jnp.sum(grad_state, axis=(0, 1))
    grad_attn_in = grad_state.astype(jnp.bfloat16)
    grad_cross_out = jnp.einsum(
        "cnw,cnd->wd", cross_flat, grad_attn_in, preferred_element_type=jnp.float32
    )
    grad_mix = jnp.einsum(
        "cnd,wd->cnw", grad_attn_in, cross_out, preferred_element_type=jnp.float32
    ).astype(jnp.bfloat16)
    cross_grads = lax.map(
        back_parts, cross_parts + (cross_max, cross_totals, split_heads(grad_mix, heads_here))
    )
    grad_query_cross = (merge_heads(cross_grads[0]).astype(jnp.float32) * scaling).astype(
        jnp.bfloat16
    )
    grad_cross_q = jnp.einsum(
        "cnd,cnw->wd", latent_norm, grad_query_cross, preferred_element_type=jnp.float32
    )
    bias_cross_q = jnp.sum(grad_query_cross.astype(jnp.float32), axis=(0, 1))
    grad_latent_in = join_back(
        jnp.einsum("cnw,wd->cnd", grad_query_cross, cross_q, preferred_element_type=jnp.float32)
    )
    unused_too, latent_pull = jax.vjp(normed, start_state, norm_gain[1], norm_bias[1])
    grad_ln_one, gain_one, shift_one = latent_pull(grad_latent_in)
    grad_latents = grad_state + grad_ln_one
    grad_pair = jnp.stack([merge_heads(cross_grads[1]), merge_heads(cross_grads[2])], axis=2)
    grad_cross_kv = jnp.einsum(
        "cld,clkw->kwd", inputs, grad_pair, preferred_element_type=jnp.float32
    )
    bias_cross_v = jnp.sum(grad_pair[:, :, 1].astype(jnp.float32), axis=(0, 1))
    arrived = lax.all_to_all(grad_pair, "head", split_axis=1, concat_axis=3, tiled=True)
    grad_share = jnp.einsum(
        "clkw,kwd->cld", arrived, weights_whole, preferred_element_type=jnp.float32
    )
    own_start = head_index * rows_here
    own_mean = lax.dynamic_slice_in_dim(row_mean, own_start, rows_here, 1)
    own_inverse = lax.dynamic_slice_in_dim(inverse, own_start, rows_here, 1)
    standard = (tokens.astype(jnp.float32) - own_mean) * own_inverse
    scaled = grad_share * norm_gain[0]
    mean_plain = jnp.mean(scaled, axis=-1, keepdims=True)
    mean_cross = jnp.mean(scaled * standard, axis=-1, keepdims=True)
    grad_tokens = (own_inverse * (scaled - mean_plain - standard * mean_cross)).astype(jnp.bfloat16)
    gain_zero, shift_zero = lax.psum(
        (jnp.sum(grad_share * standard, axis=(0, 1)), jnp.sum(grad_share, axis=(0, 1))), "head"
    )
    grad_head_bias = jnp.stack(
        [jnp.stack([bias_cross_q, bias_cross_v]), jnp.stack([bias_self_q, bias_self_v])]
    )
    grad_up_bias = jnp.stack([upbias_cross, upbias_self])
    out_full = jnp.stack(
        [jnp.stack([bias_cross_attn, bias_cross_mlp]), jnp.stack([bias_self_attn, bias_self_mlp])]
    )
    grad_out_bias = share_of(out_full, head_index, head_width)
    grad_norm_gain = share_of(
        jnp.stack([gain_zero, gain_one, gain_two, gain_three, gain_four]), head_index, head_width
    )
    grad_norm_bias = share_of(
        jnp.stack([shift_zero, shift_one, shift_two, shift_three, shift_four]),
        head_index,
        head_width,
    )
    small_sums = lax.psum(
        (grad_head_bias, grad_up_bias, grad_out_bias, grad_norm_gain, grad_norm_bias), "dp"
    )
    pieces = [
        grad_cross_q.T,
        grad_cross_kv[0].T,
        grad_cross_kv[1].T,
        grad_cross_out.T,
        grad_self_qkv[0].T,
        grad_self_qkv[1].T,
        grad_self_qkv[2].T,
        grad_self_out.T,
        grad_cross_up,
        grad_cross_down.T,
        grad_self_up,
        grad_self_down.T,
    ]
    packed = jnp.concatenate([piece.astype(jnp.bfloat16) for piece in pieces], axis=1)
    summed = lax.psum_scatter(packed, "dp", scatter_dimension=0, tiled=True).astype(jnp.float32)
    sums = []
    start = 0
    for piece in pieces:
        sums.append(summed[:, start : start + piece.shape[1]])
        start += piece.shape[1]
    return (
        latents_out,
        grad_tokens,
        grad_latents,
        sums[0].T,
        jnp.stack([sums[1].T, sums[2].T]),
        sums[3].T,
        sums[8],
        sums[9].T,
        jnp.stack([sums[4].T, sums[5].T, sums[6].T]),
        sums[7].T,
        sums[10],
        sums[11].T,
        small_sums[0],
        small_sums[1],
        small_sums[2],
        small_sums[3],
        small_sums[4],
    )


def solution(mesh):
    in_specs = (
        P("dp", "head", None),
        P("dp"),
        P("dp", None),
        P("dp", None, None),
        P("head", None),
        P(None, "head", None),
        P("head", None),
        P(None, "head"),
        P("head", None),
        P(None, "head", None),
        P("head", None),
        P(None, "head"),
        P("head", None),
        P(None, None, "head"),
        P(None, "head"),
        P(),
        P(),
        P(),
        P("dp", None, None),
    )
    out_specs = (
        P("dp", None, None),
        P("dp", "head", None),
        P("dp", None, None),
        P("head", "dp"),
        P(None, "head", "dp"),
        P("head", "dp"),
        P("dp", "head"),
        P("head", "dp"),
        P(None, "head", "dp"),
        P("head", "dp"),
        P("dp", "head"),
        P("head", "dp"),
        P(None, None, "head"),
        P(None, "head"),
        P(None, None, "head"),
        P(None, "head"),
        P(None, "head"),
    )
    return jax.shard_map(local, mesh=mesh, in_specs=in_specs, out_specs=out_specs, check_vma=False)
```

profile of v0, /device:TPU:0, one launch (start us, length us, event | category | flops | bytes accessed | tf_op | source)
XLA Modules:
  0.0 712.1 jit_solution(15768888642467319990)
XLA Ops:
  7.3 18.4 %copy.67 = bf16[1,1578,768]{2,0,1:T(2,128)(2,1)} copy(bf16[1,1578,768]{2,1,0:T(8,128)(2,1)} %param.19) | data formatting | bytes 4847616 | tf_op args[0]
  28.8 122.7 %all-gather.3.cloned.1.call-done = bf16[1,6312,768]{2,0,1:T(2,128)(2,1)} async-done(((bf16[1,1578,768]{2,0,1:T(2,128)(2,1)}), bf16[1,6312,768]{2,0,1:T(2,128)(2,1)}) %all-gather.3.cloned.1.call-update) | async-done | bytes 9695248 | tf_op jit(solution)/shard_map/all_gather | solution.py:146
  151.5 7.5 %convert_reduce_fusion = f32[6312]{0:T(1024)S(1)} fusion(bf16[1,6312,768]{2,0,1:T(2,128)(2,1)} %all-gather.3.cloned.1.call-done), kind=kLoop, calls=%fused_computation.3 | loop fusion | flops 9688920 | bytes 9720480 | tf_op jit(solution)/shard_map/reduce_sum | solution.py:150
  159.0 14.1 %fusion.4 = f32[6312]{0:T(1024)S(1)} fusion(f32[6312]{0:T(1024)S(1)} %broadcast_multiply_fusion, bf16[1,6312,768]{2,0,1:T(2,128)(2,1)} %all-gather.3.cloned.1.call-done), kind=kLoop, calls=%fused_computation.6 | loop fusion | flops 19384152 | bytes 9745728 | tf_op jit(solution)/shard_map/reduce_sum | solution.py:152
  173.2 5.6 fusion.10
  188.3 6.2 fusion.167
  201.4 31.3 %all-reduce.12.cloned.1.call-done = bf16[1,128,768]{2,1,0:T(8,128)(2,1)} async-done(((bf16[1,128,768]{2,1,0:T(8,128)(2,1)}), bf16[1,128,768]{2,1,0:T(8,128)(2,1)}) %all-reduce.12.cloned.1.call-update) | async-done | bytes 196624 | tf_op jit(solution)/shard_map/psum | solution.py:36
  239.6 30.8 %all-reduce.14.cloned.1.call-done = bf16[1,128,768]{2,1,0:T(8,128)(2,1)} async-done(((bf16[1,128,768]{2,1,0:T(8,128)(2,1)}), bf16[1,128,768]{2,1,0:T(8,128)(2,1)}) %all-reduce.14.cloned.1.call-update) | async-done | bytes 196624 | tf_op jit(solution)/shard_map/psum | solution.py:36
  280.2 32.1 %all-reduce.16.cloned.1.call-done = bf16[1,128,768]{2,1,0:T(8,128)(2,1)} async-done(((bf16[1,128,768]{2,1,0:T(8,128)(2,1)}), bf16[1,128,768]{2,1,0:T(8,128)(2,1)}) %all-reduce.16.cloned.1.call-update) | async-done | bytes 196624 | tf_op jit(solution)/shard_map/psum | solution.py:36
  320.7 32.1 %all-reduce.18.cloned.1.call-done = bf16[1,128,768]{2,1,0:T(8,128)(2,1)} async-done(((bf16[1,128,768]{2,1,0:T(8,128)(2,1)}), bf16[1,128,768]{2,1,0:T(8,128)(2,1)}) %all-reduce.18.cloned.1.call-update) | async-done | bytes 196624 | tf_op jit(solution)/shard_map/psum | solution.py:40
  369.1 32.1 %all-reduce.20.cloned.1.call-done = bf16[1,128,768]{2,1,0:T(8,128)(2,1)} async-done(((bf16[1,128,768]{2,1,0:T(8,128)(2,1)}), bf16[1,128,768]{2,1,0:T(8,128)(2,1)}) %all-reduce.20.cloned.1.call-update) | async-done | bytes 196624 | tf_op jit(solution)/shard_map/psum | solution.py:40
  412.3 29.7 %all-reduce.22.cloned.1.call-done = bf16[1,128,768]{2,1,0:T(8,128)(2,1)} async-done(((bf16[1,128,768]{2,1,0:T(8,128)(2,1)}), bf16[1,128,768]{2,1,0:T(8,128)(2,1)}) %all-reduce.22.cloned.1.call-update) | async-done | bytes 196624 | tf_op jit(solution)/shard_map/psum | solution.py:40
  449.2 11.8 %multiply_reduce_fusion = (f32[3,128]{1,0:T(4,128)S(1)}, f32[3,128,6312]{1,2,0:T(8,128)}) fusion(f32[3,128,6312]{1,2,0:T(8,128)} %get-tuple-element.268, f32[3,128]{1,0:T(4,128)S(1)} %copy-done.87, bf16[128,3,64]{0,2,1:T(8,128)(2,1)S(1)} %bitcast.305, f32[6312,3,64]{0,2,1:T(8,128)} %bitcast.281, f32[3,64]{1,0:T(4,128)S(1)} %copy-done.98), kind=kOutput, calls=%fused_computation.16 | convolution fusion | flops 319942272 | bytes 24291072 | tf_op jit(solution)/shard_map/while/body/eval_jaxpr/qhe,khe->hqk/dot_general | solution.py:67
  461.0 9.9 %multiply_convert_fusion = bf16[3,128,6312]{1,2,0:T(8,128)(2,1)} fusion(f32[3,128,6312]{1,2,0:T(8,128)} %get-tuple-element.274, f32[3,128]{1,0:T(4,128)S(1)} %get-tuple-element.273, f32[3,128,6312]{1,2,0:T(8,128)} %get-tuple-element.268, f32[3,128]{1,0:T(4,128)S(1)} %copy-done.87), kind=kLoop, calls=%fused_computation.15 | loop fusion | flops 9695232 | bytes 24241152 | tf_op jit(solution)/shard_map/while/body/eval_jaxpr/convert_element_type | solution.py:69
  478.5 6.3 convert_reduce_fusion.1
  487.9 7.9 %fusion.26 = bf16[2,192,768]{2,1,0:T(8,128)(2,1)S(1)} fusion(bf16[6312,768,1]{1,0,2:T(8,128)(2,1)} %copy-done.8, bf16[1,6312,1,192]{1,3,2,0:T(8,128)(2,1)S(1)} %bitcast.282, bf16[1,6312,1,192]{1,3,2,0:T(8,128)(2,1)S(1)} %bitcast.277), kind=kOutput, calls=%fused_computation.50 | convolution fusion | flops 3725687808 | bytes 15132672 | tf_op jit(solution)/shard_map/cld,clkw->kwd/dot_general | solution.py:273
  507.9 10.3 %copy.85 = bf16[768,4608]{1,0:T(8,128)(2,1)} copy(bf16[768,4608]{0,1:T(8,128)(2,1)} %fusion.25) | data formatting | bytes 14155776
  518.2 5.6 pad_maximum_fusion
  523.8 16.4 %copy.73 = bf16[1,6312,2,192]{3,2,0,1:T(2,128)(2,1)} copy(bf16[1,6312,2,192]{1,3,2,0:T(8,128)(2,1)} %pad_maximum_fusion) | data formatting | bytes 9695232 | tf_op jit(solution)/shard_map/stack | solution.py:272
  552.7 65.7 %all-to-all-done = bf16[1,6312,2,192]{3,2,0,1:T(2,128)(2,1)} async-done(((bf16[1,6312,2,192]{3,2,0,1:T(2,128)(2,1)}), bf16[1,6312,2,192]{3,2,0,1:T(2,128)(2,1)}, u32[]{:S(2)}, u32[]{:S(2)}) %all-to-all-start) | async-done | bytes 4847648 | tf_op jit(solution)/shard_map/all_to_all | solution.py:277
  618.4 17.0 %copy.74 = bf16[1,4,1578,2,192]{2,4,1,3,0:T(8,128)(2,1)} copy(bf16[1,4,1578,2,192]{4,3,2,1,0:T(2,128)(2,1)} %bitcast.46) | data formatting | bytes 9695232 | tf_op jit(solution)/shard_map/all_to_all | solution.py:277
  635.4 9.5 %fusion.13 = (f32[768]{0:T(1024)S(1)}, f32[1578]{0:T(1024)S(1)}, f32[1578,768,1]{1,0,2:T(8,128)S(1)}) fusion(bf16[1,1578,768]{2,1,0:T(8,128)(2,1)} %param.19, f32[1578]{0:T(1024)S(1)} %dynamic_slice.65, f32[1578]{0:T(1024)S(1)} %dynamic_slice.64, f32[768]{0:T(1024)S(1)} %copy-done.44, bf16[1578,2,768]{0,2,1:T(8,128)(2,1)} %bitcast.279, ...), kind=kOutput, calls=%fused_computation.26 | convolution fusion | flops 3732662016 | bytes 14503416 | tf_op jit(solution)/shard_map/clkw,kwd->cld/dot_general | solution.py:278
  647.8 6.2 all-reduce.2
  654.1 38.3 %all-reduce.1 = (f32[2,2,192]{2,1,0:T(2,128)}, f32[2,768]{1,0:T(2,128)}, f32[2,2,192]{2,1,0:T(2,128)}, f32[5,192]{1,0:T(8,128)}, f32[5,192]{1,0:T(8,128)}) all-reduce(f32[2,2,192]{2,1,0:T(2,128)S(1)} %pad_maximum_fusion.4, f32[2,768]{1,0:T(2,128)S(1)} %pad_maximum_fusion.3, ...), channel_id=1, replica_groups=mesh['dp'=8,'head'=4] {'dp'}, use_global_device_ids=true, to_apply=%region_39.40 | all-reduce | flops 4992 | bytes 39936 | tf_op jit(solution)/shard_map/psum | solution.py:308
  (382 shorter events, 127.9 us)
Async XLA Ops:
  7.2 230.0 %copy-start = (bf16[768,768]{1,0:T(8,128)(2,1)S(1)}, bf16[768,768]{1,0:T(8,128)(2,1)}, u32[]{:S(2)}) copy-start(bf16[768,768]{1,0:T(8,128)(2,1)} %param.27) | copy-start | bytes 3538948
  7.3 144.2 %all-gather.3.cloned.1.call-start = ((), (), s32[]{:S(2)}) async-start(), calls=%async_computation.2 | async-start | bytes 24238080 | tf_op jit(solution)/shard_map/all_gather | solution.py:146
  25.7 207.0 %all-reduce.12.cloned.1.call-start = ((), (), s32[]{:S(2)}) async-start(), calls=%async_computation.3 | async-start | bytes 393216 | tf_op jit(solution)/shard_map/psum | solution.py:36
  25.9 168.6 %copy-start.97 = (f32[3,64]{1,0:T(4,128)}, f32[3,64]{1,0:T(4,128)S(1)}, u32[]{:S(2)}) copy-start(f32[3,64]{1,0:T(4,128)S(1)} %add.328) | copy-start | bytes 2308
  27.9 131.0 %copy-start.89 = (f32[768]{0:T(1024)}, f32[768]{0:T(1024)S(1)}, u32[]{:S(2)}) copy-start(f32[768]{0:T(1024)S(1)} %get-tuple-element.220) | copy-start | bytes 9220
  27.9 207.1 %copy-start.48 = (f32[768]{0:T(1024)}, f32[768]{0:T(1024)S(1)}, u32[]{:S(2)}) copy-start(f32[768]{0:T(1024)S(1)} %get-tuple-element.219) | copy-start | bytes 9220
  28.0 130.9 %copy-start.45 = (f32[768]{0:T(1024)}, f32[768]{0:T(1024)S(1)}, u32[]{:S(2)}) copy-start(f32[768]{0:T(1024)S(1)} %get-tuple-element.215) | copy-start | bytes 9220
  28.0 145.1 %copy-start.43 = (f32[768]{0:T(1024)}, f32[768]{0:T(1024)S(1)}, u32[]{:S(2)}) copy-start(f32[768]{0:T(1024)S(1)} %get-tuple-element.216) | copy-start | bytes 9220
  28.1 130.8 %copy-start.77 = (f32[128]{0:T(128)}, f32[128]{0:T(128)S(1)}, u32[]{:S(2)}) copy-start(f32[128]{0:T(128)S(1)} %broadcast_multiply_fusion.6) | copy-start | bytes 1540
  28.4 130.6 %copy-start.101 = (f32[128]{0:T(128)}, f32[128]{0:T(128)S(1)}, u32[]{:S(2)}) copy-start(f32[128]{0:T(128)S(1)} %fusion.86) | copy-start | bytes 1540
  28.4 130.6 %copy-start.94 = (f32[128]{0:T(128)}, f32[128]{0:T(128)S(1)}, u32[]{:S(2)}) copy-start(f32[128]{0:T(128)S(1)} %fusion.133) | copy-start | bytes 1540
  28.7 154.8 %copy-start.35 = (bf16[128,192]{0,1:T(8,128)(2,1)}, bf16[128,192]{0,1:T(8,128)(2,1)S(1)}, u32[]{:S(2)}) copy-start(bf16[128,192]{0,1:T(8,128)(2,1)S(1)} %fusion.44) | copy-start | bytes 147460
  200.6 69.8 %all-reduce.14.cloned.1.call-start = ((), (), s32[]{:S(2)}) async-start(), calls=%async_computation.4 | async-start | bytes 393216 | tf_op jit(solution)/shard_map/psum | solution.py:36
  238.2 74.1 %all-reduce.16.cloned.1.call-start = ((), (), s32[]{:S(2)}) async-start(), calls=%async_computation.5 | async-start | bytes 393216 | tf_op jit(solution)/shard_map/psum | solution.py:36
  280.1 72.6 %all-reduce.18.cloned.1.call-start = ((), (), s32[]{:S(2)}) async-start(), calls=%async_computation.6 | async-start | bytes 393216 | tf_op jit(solution)/shard_map/psum | solution.py:40
  320.6 82.5 %copy-start.53 = (f32[128]{0:T(128)S(1)}, f32[128]{0:T(128)}, u32[]{:S(2)}) copy-start(f32[128]{0:T(128)} %copy-done.52) | copy-start | bytes 1540
  320.6 82.5 %copy-start.75 = (f32[128]{0:T(128)S(1)}, f32[128]{0:T(128)}, u32[]{:S(2)}) copy-start(f32[128]{0:T(128)} %copy-done.74) | copy-start | bytes 1540
  320.6 86.1 %copy-start.15 = (f32[128,768]{1,0:T(8,128)S(1)}, f32[128,768]{1,0:T(8,128)}, u32[]{:S(2)}) copy-start(f32[128,768]{1,0:T(8,128)} %copy-done.14) | copy-start | bytes 1179652
  320.6 80.6 %all-reduce.20.cloned.1.call-start = ((), (), s32[]{:S(2)}) async-start(), calls=%async_computation.7 | async-start | bytes 393216 | tf_op jit(solution)/shard_map/psum | solution.py:40
  369.1 72.9 %all-reduce.22.cloned.1.call-start = ((), (), s32[]{:S(2)}) async-start(), calls=%async_computation.8 | async-start | bytes 393216 | tf_op jit(solution)/shard_map/psum | solution.py:40
  409.8 138.4 %all-reduce.24.cloned.1.call-start = ((), (), s32[]{:S(2)}) async-start(), calls=%async_computation.11 | async-start | bytes 786432 | tf_op jit(solution)/shard_map/psum | solution.py:36
  476.8 158.6 %all-gather.5.cloned.1.call-start = ((), (), s32[]{:S(2)}) async-start(), calls=%async_computation.9 | async-start | bytes 2949120 | tf_op jit(solution)/shard_map/all_gather | solution.py:147
  477.5 220.0 %reduce-scatter.4.cloned.1.call-start = ((), (), s32[]{:S(2)}) async-start(), calls=%async_computation.10 | async-start | bytes 7962624
  540.4 78.0 %all-to-all-start = ((bf16[1,6312,2,192]{3,2,0,1:T(2,128)(2,1)}), bf16[1,6312,2,192]{3,2,0,1:T(2,128)(2,1)}, u32[]{:S(2)}, u32[]{:S(2)}) async-start(bf16[1,6312,2,192]{3,2,0,1:T(2,128)(2,1)} %copy.73), calls=%async_computation | async-start | bytes 12926976 | tf_op jit(solution)/shard_map/all_to_all | solution.py:277
  (97 other events, 1553.0 us)
Sparse Core Ops, SparseCore 0:
  25.9 125.5 all-gather.2
  200.7 32.0 all-reduce.11
  238.3 32.0 all-reduce.13
  280.3 32.0 all-reduce.15
  320.7 31.9 all-reduce.17
  369.2 32.0 all-reduce.19
  409.9 32.0 all-reduce.21
  476.9 32.9 all-reduce.23
  511.4 24.0 all-gather.4
  539.0 129.7 reduce-scatter.3
where the time goes:
time: 720 us; the launch traced here: 712 us
  waiting for transfers between devices  377 us (52%)
  matrix products  95.7 us (13%)
  local copies, waits for them, and re-layouts  86.2 us (12%)
  other arithmetic  85.1 us (12%)
  blocking collectives  44.6 us (6%)
  between operations  16.6 us (2%)
    all_gather x1, waiting for transfers between devices, local(): lax.all_gather(tokens, 'head', axis=1, tiled=True)  123 us
    psum x4, waiting for transfers between devices, join_heads(): lax.psum(partial_sum.astype(jnp.bfloat16), 'head').astype(jnp.float32)  94.3 us
    psum x3, waiting for transfers between devices, join_back(): lax.psum(partial_sum.astype(jnp.bfloat16), 'head').astype(jnp.float32)  93.9 us
    all_to_all x1, waiting for transfers between devices, local(): lax.all_to_all(grad_pair, 'head', split_axis=1, concat_axis=3, tiled=True)  65.7 us
    unnamed x232, local copies, waits for them, and re-layouts  45.2 us
    psum x1, blocking collectives, local(): lax.psum((grad_head_bias, grad_up_bias, grad_out_bias, grad_norm_gain, gr...  38.3 us
    all_to_all x1, local copies, waits for them, and re-layouts, local(): lax.all_to_all(grad_pair, 'head', split_axis=1, concat_axis=3, tiled=True)  17 us
    another operation x1, local copies, waits for them, and re-layouts, local(): jnp.stack([merge_heads(cross_grads[1]), merge_heads(cross_grads[2])], axi...  16.4 us
  transfers between devices with their start and end apart: 11, of which 8 were waited for; matrix products, arithmetic and copies ran while one was open for 15% of the time, Pallas kernels for 0%

commit v1 on v0

--- a/solution.py
+++ b/solution.py
@@ -274,7 +274,12 @@
         "cld,clkw->kwd", inputs, grad_pair, preferred_element_type=jnp.float32
     )
     bias_cross_v = jnp.sum(grad_pair[:, :, 1].astype(jnp.float32), axis=(0, 1))
-    arrived = lax.all_to_all(grad_pair, "head", split_axis=1, concat_axis=3, tiled=True)
+    arrived = jnp.concatenate(
+        lax.all_to_all(
+            jnp.stack(jnp.split(grad_pair, lax.axis_size("head"), axis=1)), "head", 0, 0
+        ),
+        axis=3,
+    )
     grad_share = jnp.einsum(
         "clkw,kwd->cld", arrived, weights_whole, preferred_element_type=jnp.float32
     )

time: 720 us -> 692 us (0.961)
  local copies, waits for them, and re-layouts: 86.2 us -> 57.8 us
    all_to_all x1 -> x0, local copies, waits for them, and re-layouts: 17 us -> none  [local(): lax.all_to_all(grad_pair, 'head', split_axis=1, concat_axis=3, tiled=True)]
    another operation x1 -> x0, local copies, waits for them, and re-layouts: 16.4 us -> none  [local(): jnp.stack([merge_heads(cross_grads[1]), merge_heads(cross_grads[2])], axi...]
    unnamed x11, waiting for transfers between devices: 0.83 us -> 14.9 us
    all_to_all x1, waiting for transfers between devices: 65.7 us -> 52 us  [local(): lax.all_to_all(jnp.stack(jnp.split(grad_pair, lax.axis_size('head'), axis...]
    unnamed x232 -> x234, local copies, waits for them, and re-layouts: 45.2 us -> 45.3 us
  transfers between devices with their start and end apart: 11 -> 11, of which waited for: 8 -> 9; matrix products, arithmetic and copies ran while one was open for 15% -> 12% of each run, Pallas kernels for 0% -> 0%
where the time goes in v1:
time: 692 us; the launch traced here: 685 us
  waiting for transfers between devices  378 us (55%)
  matrix products  94.7 us (14%)
  other arithmetic  86.6 us (13%)
  local copies, waits for them, and re-layouts  57.8 us (8%)
  blocking collectives  44.9 us (6%)
  between operations  16.6 us (2%)
    all_gather x1, waiting for transfers between devices, local(): lax.all_gather(tokens, 'head', axis=1, tiled=True)  123 us
    psum x4, waiting for transfers between devices, join_heads(): lax.psum(partial_sum.astype(jnp.bfloat16), 'head').astype(jnp.float32)  94.3 us
    psum x3, waiting for transfers between devices, join_back(): lax.psum(partial_sum.astype(jnp.bfloat16), 'head').astype(jnp.float32)  94 us
    all_to_all x1, waiting for transfers between devices, local(): lax.all_to_all(jnp.stack(jnp.split(grad_pair, lax.axis_size('head'), axis...  52 us
    unnamed x234, local copies, waits for them, and re-layouts  45.3 us
    psum x1, blocking collectives, local(): lax.psum((grad_head_bias, grad_up_bias, grad_out_bias, grad_norm_gain, gr...  38.8 us
    unnamed x11, waiting for transfers between devices  14.9 us
    reduce_sum x1, other arithmetic, local(): jnp.mean(centered * centered, axis=-1, keepdims=True) + EPSILON  14.1 us
  transfers between devices with their start and end apart: 11, of which 9 were waited for; matrix products, arithmetic and copies ran while one was open for 12% of the time, Pallas kernels for 0%

profile of v1, /device:TPU:0, one launch (start us, length us, event | category | flops | bytes accessed | tf_op | source)
XLA Modules:
  0.0 684.8 jit_solution(6974735285664845739)
XLA Ops:
  7.3 18.4 %copy.66 = bf16[1,1578,768]{2,0,1:T(2,128)(2,1)} copy(bf16[1,1578,768]{2,1,0:T(8,128)(2,1)} %param.19) | data formatting | bytes 4847616 | tf_op args[0]
  28.8 122.7 %all-gather.3.cloned.1.call-done = bf16[1,6312,768]{2,0,1:T(2,128)(2,1)} async-done(((bf16[1,1578,768]{2,0,1:T(2,128)(2,1)}), bf16[1,6312,768]{2,0,1:T(2,128)(2,1)}) %all-gather.3.cloned.1.call-update) | async-done | bytes 9695248 | tf_op jit(solution)/shard_map/all_gather | solution.py:146
  151.5 7.5 %convert_reduce_fusion = f32[6312]{0:T(1024)S(1)} fusion(bf16[1,6312,768]{2,0,1:T(2,128)(2,1)} %all-gather.3.cloned.1.call-done), kind=kLoop, calls=%fused_computation.3 | loop fusion | flops 9688920 | bytes 9720480 | tf_op jit(solution)/shard_map/reduce_sum | solution.py:150
  159.0 14.1 %fusion.4 = f32[6312]{0:T(1024)S(1)} fusion(f32[6312]{0:T(1024)S(1)} %broadcast_multiply_fusion, bf16[1,6312,768]{2,0,1:T(2,128)(2,1)} %all-gather.3.cloned.1.call-done), kind=kLoop, calls=%fused_computation.6 | loop fusion | flops 19384152 | bytes 9745728 | tf_op jit(solution)/shard_map/reduce_sum | solution.py:152
  173.2 5.6 fusion.10
  188.3 6.2 fusion.177
  201.4 31.3 %all-reduce.12.cloned.1.call-done = bf16[1,128,768]{2,1,0:T(8,128)(2,1)} async-done(((bf16[1,128,768]{2,1,0:T(8,128)(2,1)}), bf16[1,128,768]{2,1,0:T(8,128)(2,1)}) %all-reduce.12.cloned.1.call-update) | async-done | bytes 196624 | tf_op jit(solution)/shard_map/psum | solution.py:36
  239.6 30.8 %all-reduce.14.cloned.1.call-done = bf16[1,128,768]{2,1,0:T(8,128)(2,1)} async-done(((bf16[1,128,768]{2,1,0:T(8,128)(2,1)}), bf16[1,128,768]{2,1,0:T(8,128)(2,1)}) %all-reduce.14.cloned.1.call-update) | async-done | bytes 196624 | tf_op jit(solution)/shard_map/psum | solution.py:36
  280.2 32.1 %all-reduce.16.cloned.1.call-done = bf16[1,128,768]{2,1,0:T(8,128)(2,1)} async-done(((bf16[1,128,768]{2,1,0:T(8,128)(2,1)}), bf16[1,128,768]{2,1,0:T(8,128)(2,1)}) %all-reduce.16.cloned.1.call-update) | async-done | bytes 196624 | tf_op jit(solution)/shard_map/psum | solution.py:36
  320.7 32.1 %all-reduce.18.cloned.1.call-done = bf16[1,128,768]{2,1,0:T(8,128)(2,1)} async-done(((bf16[1,128,768]{2,1,0:T(8,128)(2,1)}), bf16[1,128,768]{2,1,0:T(8,128)(2,1)}) %all-reduce.18.cloned.1.call-update) | async-done | bytes 196624 | tf_op jit(solution)/shard_map/psum | solution.py:40
  369.1 32.1 %all-reduce.20.cloned.1.call-done = bf16[1,128,768]{2,1,0:T(8,128)(2,1)} async-done(((bf16[1,128,768]{2,1,0:T(8,128)(2,1)}), bf16[1,128,768]{2,1,0:T(8,128)(2,1)}) %all-reduce.20.cloned.1.call-update) | async-done | bytes 196624 | tf_op jit(solution)/shard_map/psum | solution.py:40
  412.3 29.7 %all-reduce.22.cloned.1.call-done = bf16[1,128,768]{2,1,0:T(8,128)(2,1)} async-done(((bf16[1,128,768]{2,1,0:T(8,128)(2,1)}), bf16[1,128,768]{2,1,0:T(8,128)(2,1)}) %all-reduce.22.cloned.1.call-update) | async-done | bytes 196624 | tf_op jit(solution)/shard_map/psum | solution.py:40
  449.2 11.8 %multiply_reduce_fusion = (f32[3,128]{1,0:T(4,128)S(1)}, f32[3,128,6312]{1,2,0:T(8,128)}) fusion(f32[3,128,6312]{1,2,0:T(8,128)} %get-tuple-element.272, f32[3,128]{1,0:T(4,128)S(1)} %copy-done.87, bf16[128,3,64]{0,2,1:T(8,128)(2,1)S(1)} %bitcast.311, f32[6312,3,64]{0,2,1:T(8,128)} %bitcast.287, f32[3,64]{1,0:T(4,128)S(1)} %copy-done.98), kind=kOutput, calls=%fused_computation.16 | convolution fusion | flops 319942272 | bytes 24291072 | tf_op jit(solution)/shard_map/while/body/eval_jaxpr/qhe,khe->hqk/dot_general | solution.py:67
  461.0 9.9 %multiply_convert_fusion = bf16[3,128,6312]{1,2,0:T(8,128)(2,1)} fusion(f32[3,128,6312]{1,2,0:T(8,128)} %get-tuple-element.278, f32[3,128]{1,0:T(4,128)S(1)} %get-tuple-element.277, f32[3,128,6312]{1,2,0:T(8,128)} %get-tuple-element.272, f32[3,128]{1,0:T(4,128)S(1)} %copy-done.87), kind=kLoop, calls=%fused_computation.15 | loop fusion | flops 9695232 | bytes 24241152 | tf_op jit(solution)/shard_map/while/body/eval_jaxpr/convert_element_type | solution.py:69
  482.8 7.0 %convert_reduce_fusion.1 = (f32[3,64]{1,0:T(4,128)}, bf16[3,64,6312]{2,1,0:T(8,128)(2,1)S(1)}) fusion(bf16[128,3,64]{0,2,1:T(8,128)(2,1)S(1)} %bitcast.312, f32[3,128,6312]{1,2,0:T(8,128)} %get-tuple-element.272, f32[3,128]{1,0:T(4,128)S(1)} %copy-done.87), kind=kOutput, calls=%fused_computation.32 | convolution fusion | flops 318730560 | bytes 12170496 | tf_op jit(solution)/shard_map/while/body/eval_jaxpr/hqk,qhe->khe/dot_general | solution.py:64
  507.3 10.3 %copy.83 = bf16[768,4608]{1,0:T(8,128)(2,1)} copy(bf16[768,4608]{0,1:T(8,128)(2,1)} %fusion.26) | data formatting | bytes 14155776
  524.8 5.2 all-to-all-start
  536.9 52.0 %all-to-all-done = bf16[4,1,1578,2,192]{2,4,3,1,0:T(8,128)(2,1)} async-done(((bf16[4,1,1578,2,192]{2,4,3,1,0:T(8,128)(2,1)}), bf16[4,1,1578,2,192]{2,4,3,1,0:T(8,128)(2,1)}, u32[]{:S(2)}, u32[]{:S(2)}) %all-to-all-start) | async-done | bytes 4847648 | tf_op jit(solution)/shard_map/all_to_all | solution.py:278
  588.9 5.1 copy.72
  593.9 9.2 %fusion.14 = (f32[768]{0:T(1024)S(1)}, f32[1578]{0:T(1024)S(1)}, f32[1578,768,1]{1,0,2:T(8,128)S(1)}) fusion(bf16[1,1578,768]{2,1,0:T(8,128)(2,1)} %param.19, f32[1578]{0:T(1024)S(1)} %dynamic_slice.65, f32[1578]{0:T(1024)S(1)} %dynamic_slice.64, f32[768]{0:T(1024)S(1)} %copy-done.44, bf16[1578,2,768]{0,2,1:T(8,128)(2,1)} %bitcast.285, ...), kind=kOutput, calls=%fused_computation.35 | convolution fusion | flops 3732662016 | bytes 14503416 | tf_op jit(solution)/shard_map/clkw,kwd->cld/dot_general | solution.py:283
  606.0 6.1 all-reduce.2
  612.3 38.8 %all-reduce.1 = (f32[2,2,192]{2,1,0:T(2,128)}, f32[2,768]{1,0:T(2,128)}, f32[2,2,192]{2,1,0:T(2,128)}, f32[5,192]{1,0:T(8,128)}, f32[5,192]{1,0:T(8,128)}) all-reduce(f32[2,2,192]{2,1,0:T(2,128)S(1)} %pad_maximum_fusion.5, f32[2,768]{1,0:T(2,128)S(1)} %pad_maximum_fusion.4, ...), channel_id=1, replica_groups=mesh['dp'=8,'head'=4] {'dp'}, use_global_device_ids=true, to_apply=%region_39.40 | all-reduce | flops 4992 | bytes 39936 | tf_op jit(solution)/shard_map/psum | solution.py:313
  651.1 5.0 fusion.17
  656.1 14.1 %reduce-scatter.4.cloned.1.call-done = bf16[96,4608]{1,0:T(8,128)(2,1)} async-done(((bf16[768,4608]{1,0:T(8,128)(2,1)}), bf16[96,4608]{1,0:T(8,128)(2,1)}) %reduce-scatter.4.cloned.1.call-update) | async-done | bytes 884752
  (384 shorter events, 131.0 us)
Async XLA Ops:
  7.2 230.0 %copy-start = (bf16[768,768]{1,0:T(8,128)(2,1)S(1)}, bf16[768,768]{1,0:T(8,128)(2,1)}, u32[]{:S(2)}) copy-start(bf16[768,768]{1,0:T(8,128)(2,1)} %param.27) | copy-start | bytes 3538948
  7.3 144.2 %all-gather.3.cloned.1.call-start = ((), (), s32[]{:S(2)}) async-start(), calls=%async_computation.2 | async-start | bytes 24238080 | tf_op jit(solution)/shard_map/all_gather | solution.py:146
  25.7 207.0 %all-reduce.12.cloned.1.call-start = ((), (), s32[]{:S(2)}) async-start(), calls=%async_computation.3 | async-start | bytes 393216 | tf_op jit(solution)/shard_map/psum | solution.py:36
  25.9 168.6 %copy-start.97 = (f32[3,64]{1,0:T(4,128)}, f32[3,64]{1,0:T(4,128)S(1)}, u32[]{:S(2)}) copy-start(f32[3,64]{1,0:T(4,128)S(1)} %add.328) | copy-start | bytes 2308
  27.9 131.0 %copy-start.89 = (f32[768]{0:T(1024)}, f32[768]{0:T(1024)S(1)}, u32[]{:S(2)}) copy-start(f32[768]{0:T(1024)S(1)} %get-tuple-element.220) | copy-start | bytes 9220
  27.9 207.1 %copy-start.48 = (f32[768]{0:T(1024)}, f32[768]{0:T(1024)S(1)}, u32[]{:S(2)}) copy-start(f32[768]{0:T(1024)S(1)} %get-tuple-element.219) | copy-start | bytes 9220
  28.0 130.9 %copy-start.45 = (f32[768]{0:T(1024)}, f32[768]{0:T(1024)S(1)}, u32[]{:S(2)}) copy-start(f32[768]{0:T(1024)S(1)} %get-tuple-element.215) | copy-start | bytes 9220
  28.0 145.1 %copy-start.43 = (f32[768]{0:T(1024)}, f32[768]{0:T(1024)S(1)}, u32[]{:S(2)}) copy-start(f32[768]{0:T(1024)S(1)} %get-tuple-element.216) | copy-start | bytes 9220
  28.1 130.8 %copy-start.77 = (f32[128]{0:T(128)}, f32[128]{0:T(128)S(1)}, u32[]{:S(2)}) copy-start(f32[128]{0:T(128)S(1)} %broadcast_multiply_fusion.6) | copy-start | bytes 1540
  28.4 130.6 %copy-start.101 = (f32[128]{0:T(128)}, f32[128]{0:T(128)S(1)}, u32[]{:S(2)}) copy-start(f32[128]{0:T(128)S(1)} %fusion.95) | copy-start | bytes 1540
  28.4 130.6 %copy-start.94 = (f32[128]{0:T(128)}, f32[128]{0:T(128)S(1)}, u32[]{:S(2)}) copy-start(f32[128]{0:T(128)S(1)} %fusion.142) | copy-start | bytes 1540
  28.7 154.8 %copy-start.35 = (bf16[128,192]{0,1:T(8,128)(2,1)}, bf16[128,192]{0,1:T(8,128)(2,1)S(1)}, u32[]{:S(2)}) copy-start(bf16[128,192]{0,1:T(8,128)(2,1)S(1)} %fusion.53) | copy-start | bytes 147460
  200.6 69.8 %all-reduce.14.cloned.1.call-start = ((), (), s32[]{:S(2)}) async-start(), calls=%async_computation.4 | async-start | bytes 393216 | tf_op jit(solution)/shard_map/psum | solution.py:36
  238.2 74.1 %all-reduce.16.cloned.1.call-start = ((), (), s32[]{:S(2)}) async-start(), calls=%async_computation.5 | async-start | bytes 393216 | tf_op jit(solution)/shard_map/psum | solution.py:36
  280.1 72.6 %all-reduce.18.cloned.1.call-start = ((), (), s32[]{:S(2)}) async-start(), calls=%async_computation.6 | async-start | bytes 393216 | tf_op jit(solution)/shard_map/psum | solution.py:40
  320.6 82.6 %copy-start.53 = (f32[128]{0:T(128)S(1)}, f32[128]{0:T(128)}, u32[]{:S(2)}) copy-start(f32[128]{0:T(128)} %copy-done.52) | copy-start | bytes 1540
  320.6 82.6 %copy-start.75 = (f32[128]{0:T(128)S(1)}, f32[128]{0:T(128)}, u32[]{:S(2)}) copy-start(f32[128]{0:T(128)} %copy-done.74) | copy-start | bytes 1540
  320.6 86.1 %copy-start.15 = (f32[128,768]{1,0:T(8,128)S(1)}, f32[128,768]{1,0:T(8,128)}, u32[]{:S(2)}) copy-start(f32[128,768]{1,0:T(8,128)} %copy-done.14) | copy-start | bytes 1179652
  320.6 80.7 %all-reduce.20.cloned.1.call-start = ((), (), s32[]{:S(2)}) async-start(), calls=%async_computation.7 | async-start | bytes 393216 | tf_op jit(solution)/shard_map/psum | solution.py:40
  369.1 72.9 %all-reduce.22.cloned.1.call-start = ((), (), s32[]{:S(2)}) async-start(), calls=%async_computation.8 | async-start | bytes 393216 | tf_op jit(solution)/shard_map/psum | solution.py:40
  409.8 122.5 %all-reduce.24.cloned.1.call-start = ((), (), s32[]{:S(2)}) async-start(), calls=%async_computation.11 | async-start | bytes 786432 | tf_op jit(solution)/shard_map/psum | solution.py:36
  476.8 117.1 %all-gather.5.cloned.1.call-start = ((), (), s32[]{:S(2)}) async-start(), calls=%async_computation.9 | async-start | bytes 2949120 | tf_op jit(solution)/shard_map/all_gather | solution.py:147
  477.5 192.6 %reduce-scatter.4.cloned.1.call-start = ((), (), s32[]{:S(2)}) async-start(), calls=%async_computation.10 | async-start | bytes 7962624
  524.8 64.1 %all-to-all-start = ((bf16[4,1,1578,2,192]{2,4,3,1,0:T(8,128)(2,1)}), bf16[4,1,1578,2,192]{2,4,3,1,0:T(8,128)(2,1)}, u32[]{:S(2)}, u32[]{:S(2)}) async-start(bf16[4,1,1578,2,192]{2,4,3,1,0:T(8,128)(2,1)} %pad_maximum_fusion.1), calls=%async_computation | async-start | bytes 10223616 | tf_op jit(solution)/shard_map/all_to_all | solution.py:278
  (98 other events, 1545.0 us)
Sparse Core Ops, SparseCore 0:
  25.9 125.5 all-gather.2
  200.7 32.0 all-reduce.11
  238.3 32.0 all-reduce.13
  280.3 32.0 all-reduce.15
  320.7 32.0 all-reduce.17
  369.2 32.0 all-reduce.19
  410.0 32.0 all-reduce.21
  476.9 32.9 all-reduce.23
  511.4 24.8 all-gather.4
  539.9 130.2 reduce-scatter.3
